TPU v7x, 256 devices: a whole 4x4x8 slice. The times are simulated.
256 devices in a mesh: vocab: 32 (over z_lo, x, core), seq: 8 (over y, z_hi).
Axes of the slice: x: 4, y: 4, z: 8 (z_hi: 2, z_lo: 4; z = z_hi * 4 + z_lo), core: 2. Of those that a mesh axis runs over, the one named last changes fastest.
Arguments:
- hidden_states: bfloat16 [2048, 3584], P('seq', 'vocab'), may hold values from -6 to 6
- norm_gain: float32 [3584], replicated, may hold values from 0.5 to 1.5
- embedding: bfloat16 [256000, 3584], P(('vocab', 'seq')), may hold values from -0.29882812 to 0.29882812
- targets: int32 [2048], replicated, may hold values from 0 to 255999
Outputs:
- token_loss: float32 [2048], P('seq')
- mean_loss: float32 [], replicated
All inputs are finite; a program needn't handle non-finite values.
Results may differ from a plain program's by a relative error of at most 0.0005.
Values may be sent and summed in bfloat16 or wider, within the bound.
No kernel may reach another device: no remote copies, remote signals or barrier semaphores. Data moves between devices by JAX's collectives and lax.ppermute only.
A program may use at most 64 MiB of HBM per device.

v0:
```python
import jax
import jax.numpy as jnp
from jax import lax
from jax.sharding import Mesh
from jax.sharding import PartitionSpec as P

SEQ = ("seq_0", "seq_1")
VOCAB_SEQ = ("vocab", "seq_0", "seq_1")


def gathered_by_axis(x, axes, dim):
    if not axes:
        return x
    nearer = lax.all_gather(x, axes[-1], axis=dim, tiled=True)
    return gathered_by_axis(nearer, axes[:-1], dim)


def split_up(x, dim, length):
    dims = x.shape
    pieces = x.reshape(*dims[:dim], length, dims[dim] // length, *dims[dim + 1 :])
    return jnp.moveaxis(pieces, dim, 0)


def summed_on_arrival(x, axis, dim):
    pieces = split_up(x, dim, lax.axis_size(axis))
    arrived = lax.all_to_all(pieces, axis, split_axis=0, concat_axis=0, tiled=True)
    return arrived.sum(axis=0)


def copy_for_each(x, axis):
    copies = jnp.broadcast_to(x, (lax.axis_size(axis), *x.shape))
    return lax.all_to_all(copies, axis, split_axis=0, concat_axis=0, tiled=True)


def over_copies(x, axis):
    return copy_for_each(x, axis).sum(axis=0)


def in_one(arrays, axis):
    vector, at, outs = (jnp.concatenate([a.reshape(-1) for a in arrays]), 0, [])
    running = over_copies(vector, axis)
    for a in arrays:
        outs.append(running[at : at + a.size].reshape(a.shape))
        at += a.size
    return tuple(outs)


def normalize(rows, norm_gain):
    values = rows.astype(jnp.float32)
    meansq = jnp.mean(values * values, axis=-1, keepdims=True)
    return (values * lax.rsqrt(meansq + 1e-06) * norm_gain).astype(jnp.bfloat16)


def vocab_terms_of(embedding, targets, normed_rows):
    local_rows = embedding.shape[0]
    base = (lax.axis_index("vocab") * lax.axis_size(SEQ) + lax.axis_index(SEQ)) * local_rows
    scores = jnp.einsum("vd,td->vt", embedding, normed_rows, preferred_element_type=jnp.float32)
    capped = 30.0 * jnp.tanh(scores / 30.0)
    total = jnp.sum(jnp.exp(capped), axis=0)
    ids = base + jnp.arange(local_rows, dtype=jnp.int32)
    hit = ids[:, None] == targets[None, :]
    picked = jnp.sum(jnp.where(hit, capped, 0.0), axis=0)
    return (total, picked)


def local(hidden_states, norm_gain, embedding, targets):
    all_count = targets.shape[0]
    gathered_rows = gathered_by_axis(hidden_states, SEQ, 0)
    whole = lax.all_gather(gathered_rows, "vocab", axis=1, tiled=True)
    normed = normalize(whole, norm_gain)
    total, picked = vocab_terms_of(embedding, targets, normed)
    total, picked = (summed_on_arrival(total, SEQ, 0), summed_on_arrival(picked, SEQ, 0))
    total, picked = in_one((total, picked), "vocab")
    token_loss = jnp.log(total) - picked
    mean_loss = over_copies(jnp.sum(token_loss), SEQ) / all_count
    return (token_loss, mean_loss)


def solution(mesh):
    torus = Mesh(mesh.devices.reshape(mesh.shape["vocab"], 4, 2), ("vocab", "seq_0", "seq_1"))
    placed = (P(SEQ, "vocab"), P(), P(VOCAB_SEQ, None), P())
    return jax.shard_map(
        local, mesh=torus, in_specs=placed, out_specs=(P(SEQ), P()), check_vma=False
    )
```

profile of v0, /device:TPU:1, one launch (start us, length us, event | category | flops | bytes accessed | tf_op | source)
XLA Modules:
  0.0 223.2 jit_solution(5389422925406586718)
XLA Ops:
  7.2 0.0 copy-start.1
  7.2 0.0 copy-start
  7.2 0.0 all-gather.2.cloned.1.call-start
  7.2 10.2 %all_gather.9 = bf16[512,112]{0,1:T(8,128)(2,1)S(1)} all-gather(bf16[256,112]{0,1:T(8,128)(2,1)} %param.4), channel_id=1, replica_groups=mesh['vocab'=32,'seq_0'=4,'seq_1'=2] {'seq_1'}, dimensions={0}, use_global_device_ids=true | all-gather | bytes 172032 | tf_op jit(solution)/shard_map/all_gather | solution.py:14
  17.5 12.0 %all_gather.10 = bf16[2048,112]{0,1:T(8,128)(2,1)} all-gather(bf16[512,112]{0,1:T(8,128)(2,1)S(1)} %all_gather.9), channel_id=1, replica_groups=mesh['vocab'=32,'seq_0'=4,'seq_1'=2] {'seq_0'}, dimensions={0}, use_global_device_ids=true | all-gather | bytes 573440 | tf_op jit(solution)/shard_map/all_gather | solution.py:14
  29.5 0.0 all-gather.2.cloned.1.call-update
  29.5 94.2 %all-gather.2.cloned.1.call-done = bf16[2048,3584]{0,1:T(8,128)(2,1)} async-done(((bf16[2048,112]{0,1:T(8,128)(2,1)}), bf16[2048,3584]{0,1:T(8,128)(2,1)}) %all-gather.2.cloned.1.call-update) | async-done | bytes 14680080 | tf_op jit(solution)/shard_map/all_gather | solution.py:69
  123.7 8.1 %fusion = f32[2048]{0:T(1024)S(1)} fusion(bf16[2048,3584]{0,1:T(8,128)(2,1)} %all-gather.2.cloned.1.call-done), kind=kLoop, calls=%fused_computation.2 | loop fusion | flops 22018048 | bytes 14688256 | tf_op jit(solution)/shard_map/reduce_sum | solution.py:50
  131.8 0.0 copy-done.1
  131.8 0.0 copy-done
  131.8 24.3 %fusion.7 = (f32[2048]{0:T(1024)}, f32[2048]{0:T(1024)S(1)}) fusion(s32[2048]{0:T(1024)S(1)} %copy-done.1, s32[1000]{0:T(1024)S(1)} %iota_add_fusion, bf16[1000,3584]{1,0:T(8,128)(2,1)} %param.6, bf16[2048,3584]{0,1:T(8,128)(2,1)} %all-gather.2.cloned.1.call-done, f32[3584]{0:T(1024)S(1)} %copy-done, f32[2048]{0:T(1024)S(1)} %add_rsqrt_fusion), kind=kOutput, calls=%fused_computation.10 | convolution fusion | flops 14721708032 | bytes 21899168 | tf_op jit(solution)/shard_map/vd,td->vt/dot_general | solution.py:57
  156.0 17.8 %all_to_all.30 = f32[8,1,256]{2,1,0:T(1,128)S(1)} all-to-all(f32[8,1,256]{2,1,0:T(1,128)S(1)} %bitcast.10), channel_id=1, replica_groups=mesh['vocab'=32,'seq_0'=4,'seq_1'=2] {'seq_0','seq_1'}, dimensions={0} | all-to-all | bytes 16384 | tf_op jit(solution)/shard_map/all_to_all | solution.py:26
  173.8 3.3 %all-to-all-start = ((f32[8,1,256]{2,1,0:T(1,128)}), f32[8,1,256]{2,1,0:T(1,128)S(1)}, u32[]{:S(2)}, u32[]{:S(2)}) async-start(f32[8,1,256]{2,1,0:T(1,128)} %bitcast.1), calls=%async_computation | async-start | bytes 16384 | tf_op jit(solution)/shard_map/all_to_all | solution.py:26
  177.1 8.8 %all-to-all-done = f32[8,1,256]{2,1,0:T(1,128)S(1)} async-done(((f32[8,1,256]{2,1,0:T(1,128)}), f32[8,1,256]{2,1,0:T(1,128)S(1)}, u32[]{:S(2)}, u32[]{:S(2)}) %all-to-all-start) | async-done | bytes 8224 | tf_op jit(solution)/shard_map/all_to_all | solution.py:26
  186.1 14.7 %all_to_all.31 = f32[32,1,512]{2,1,0:T(1,128)S(1)} all-to-all(f32[32,1,512]{2,1,0:T(1,128)S(1)} %broadcast_in_dim.15), channel_id=1, replica_groups=mesh['vocab'=32,'seq_0'=4,'seq_1'=2] {'vocab'}, dimensions={0} | all-to-all | bytes 131072 | tf_op jit(solution)/shard_map/all_to_all | solution.py:32
  200.8 0.1 reduce_sum.77
  200.8 1.2 fusion.9
  202.0 0.6 broadcast_in_dim.16
  202.7 11.3 %all_to_all.32 = f32[8,1,1]{2,1,0:T(1,128)S(1)} all-to-all(f32[8,1,1]{2,1,0:T(1,128)S(1)} %broadcast_in_dim.16), channel_id=1, replica_groups=mesh['vocab'=32,'seq_0'=4,'seq_1'=2] {'seq_0','seq_1'}, dimensions={0} | all-to-all | bytes 64 | tf_op jit(solution)/shard_map/all_to_all | solution.py:32
  214.0 0.6 reduce_sum.79
  (6 shorter events, 0.1 us)
Async XLA Ops:
  7.2 124.6 %copy-start.1 = (s32[2048]{0:T(1024)S(1)}, s32[2048]{0:T(1024)}, u32[]{:S(2)}) copy-start(s32[2048]{0:T(1024)} %param.7) | copy-start | bytes 24580
  7.2 124.6 %copy-start = (f32[3584]{0:T(1024)S(1)}, f32[3584]{0:T(1024)}, u32[]{:S(2)}) copy-start(f32[3584]{0:T(1024)} %param.5) | copy-start | bytes 43012
  7.2 116.5 %all-gather.2.cloned.1.call-start = ((), (), s32[]{:S(2)}) async-start(), calls=%async_computation.4 | async-start | bytes 15138816 | tf_op jit(solution)/shard_map/all_gather | solution.py:69
  173.8 12.2 %all-to-all-start = ((f32[8,1,256]{2,1,0:T(1,128)}), f32[8,1,256]{2,1,0:T(1,128)S(1)}, u32[]{:S(2)}, u32[]{:S(2)}) async-start(f32[8,1,256]{2,1,0:T(1,128)} %bitcast.1), calls=%async_computation | async-start | bytes 16384 | tf_op jit(solution)/shard_map/all_to_all | solution.py:26
Sparse Core Ops, SparseCore 0:
  29.6 94.0 all-gather.1
where the time goes:
time: 224 us; the launch traced here: 223 us
  waiting for transfers between devices  103 us (46%)
  blocking collectives  66 us (29%)
  matrix products  24.3 us (11%)
  between operations  15.9 us (7%)
  other arithmetic  10 us (4%)
  starting transfers between devices  3.36 us (2%)
    all_gather x1, waiting for transfers between devices, local(): whole = lax.all_gather(gathered_rows, 'vocab', axis=1, tiled=True)  94.2 us
    all_to_all x2, blocking collectives, copy_for_each(): return lax.all_to_all(copies, axis, split_axis=0, concat_axis=0, tiled=True)  26 us
    dot_general x1, matrix products, vocab_terms_of(): jnp.einsum('vd,td->vt', embedding, normed_rows, preferred_element_type=jn...  24.3 us
    all_gather x2, blocking collectives, gathered_by_axis(): nearer = lax.all_gather(x, axes[-1], axis=dim, tiled=True)  22.2 us
    all_to_all x1, blocking collectives, summed_on_arrival(): lax.all_to_all(pieces, axis, split_axis=0, concat_axis=0, tiled=True)  17.8 us
    all_to_all x1, waiting for transfers between devices, summed_on_arrival(): lax.all_to_all(pieces, axis, split_axis=0, concat_axis=0, tiled=True)  8.85 us
    reduce_sum x1, other arithmetic, normalize(): meansq = jnp.mean(values * values, axis=-1, keepdims=True)  8.09 us
  transfers between devices with their start and end apart: 2, of which 2 were waited for; matrix products, arithmetic and copies ran while one was open for 0% of the time, Pallas kernels for 0%

commit v1 on v0

--- a/solution.py
+++ b/solution.py
@@ -66,7 +66,12 @@
 def local(hidden_states, norm_gain, embedding, targets):
     all_count = targets.shape[0]
     gathered_rows = gathered_by_axis(hidden_states, SEQ, 0)
-    whole = lax.all_gather(gathered_rows, "vocab", axis=1, tiled=True)
+    pile = []
+    for _ in range(lax.psum(1, axis_name="vocab")):
+        pile.append(gathered_rows)
+    b_next = jnp.stack(pile)
+    local_out = lax.all_to_all(b_next, "vocab", 0, 0)
+    whole = jnp.concatenate(local_out, 1)
     normed = normalize(whole, norm_gain)
     total, picked = vocab_terms_of(embedding, targets, normed)
     total, picked = (summed_on_arrival(total, SEQ, 0), summed_on_arrival(picked, SEQ, 0))

time: 224 us -> 465 us (2.08)
  waiting for transfers between devices: 103 us -> 335 us
  between operations: 15.9 us -> 2.49 us
  starting transfers between devices: 3.36 us -> 15 us
  other arithmetic: 10 us -> 17.1 us
  local copies, waits for them, and re-layouts: 0.69 us -> 7.78 us
    all_to_all x0 -> x1, waiting for transfers between devices: none -> 326 us  [local(): local_out = lax.all_to_all(b_next, 'vocab', 0, 0)]
    all_gather x1 -> x0, waiting for transfers between devices: 94.2 us -> none  [local(): whole = lax.all_gather(gathered_rows, 'vocab', axis=1, tiled=True)]
    all_to_all x0 -> x1, starting transfers between devices: none -> 11.6 us  [local(): local_out = lax.all_to_all(b_next, 'vocab', 0, 0)]
    another operation x0 -> x1, local copies, waits for them, and re-layouts: none -> 7.08 us  [local(): b_next = jnp.stack(pile)]
    convert_element_type x0 -> x1, other arithmetic: none -> 7.05 us  [normalize(): return (values * lax.rsqrt(meansq + 1e-06) * norm_gain).astype(jnp.bfloat16)]
where the time goes in v1:
time: 465 us
  waiting for transfers between devices  335 us (72%)
  blocking collectives  66.7 us (14%)
  matrix products  21.1 us (5%)
  other arithmetic  17.1 us (4%)
  starting transfers between devices  15 us (3%)
  local copies, waits for them, and re-layouts  7.78 us (2%)
    all_to_all x1, waiting for transfers between devices, local(): local_out = lax.all_to_all(b_next, 'vocab', 0, 0)  326 us
    all_to_all x2, blocking collectives, copy_for_each(): return lax.all_to_all(copies, axis, split_axis=0, concat_axis=0, tiled=True)  25.3 us
    dot_general x1, matrix products, vocab_terms_of(): jnp.einsum('vd,td->vt', embedding, normed_rows, preferred_element_type=jn...  21.1 us
    all_gather x2, blocking collectives, gathered_by_axis(): nearer = lax.all_gather(x, axes[-1], axis=dim, tiled=True)  21 us
    all_to_all x1, blocking collectives, summed_on_arrival(): lax.all_to_all(pieces, axis, split_axis=0, concat_axis=0, tiled=True)  20.4 us
    all_to_all x1, starting transfers between devices, local(): local_out = lax.all_to_all(b_next, 'vocab', 0, 0)  11.6 us
  transfers between devices with their start and end apart: 2, of which 2 were waited for; matrix products, arithmetic and copies ran while one was open for 0% of the time, Pallas kernels for 0%

profile of v1, /device:TPU:1, one launch (start us, length us, event | category | flops | bytes accessed | tf_op | source)
XLA Modules:
  0.0 464.7 jit_solution(12748186865320753039)
XLA Ops:
  0.6 10.2 %all_gather.6 = bf16[512,112]{0,1:T(8,128)(2,1)S(1)} all-gather(bf16[256,112]{0,1:T(8,128)(2,1)} %param.4), channel_id=1, replica_groups=mesh['vocab'=32,'seq_0'=4,'seq_1'=2] {'seq_1'}, dimensions={0}, use_global_device_ids=true | all-gather | bytes 172032 | tf_op jit(solution)/shard_map/all_gather | solution.py:14
  10.9 10.8 %all_gather.7 = bf16[2048,112]{0,1:T(8,128)(2,1)S(1)} all-gather(bf16[512,112]{0,1:T(8,128)(2,1)S(1)} %all_gather.6), channel_id=1, replica_groups=mesh['vocab'=32,'seq_0'=4,'seq_1'=2] {'seq_0'}, dimensions={0}, use_global_device_ids=true | all-gather | bytes 573440 | tf_op jit(solution)/shard_map/all_gather | solution.py:14
  21.6 7.1 %stack.2 = bf16[32,2048,112]{1,2,0:T(8,128)(2,1)} broadcast(bf16[2048,112]{0,1:T(8,128)(2,1)S(1)} %all_gather.7), dimensions={1,2} | broadcast | bytes 15138816 | tf_op jit(solution)/shard_map/stack | solution.py:72
  28.7 11.6 %all-to-all-start = ((bf16[32,2048,112]{1,2,0:T(8,128)(2,1)}), bf16[32,2048,112]{1,2,0:T(8,128)(2,1)}, u32[]{:S(2)}, u32[]{:S(2)}) async-start(bf16[32,2048,112]{1,2,0:T(8,128)(2,1)} %stack.2), calls=%async_computation | async-start | bytes 29360128 | tf_op jit(solution)/shard_map/all_to_all | solution.py:73
  40.4 0.0 copy-start
  40.4 325.7 %all-to-all-done = bf16[32,2048,112]{1,2,0:T(8,128)(2,1)} async-done(((bf16[32,2048,112]{1,2,0:T(8,128)(2,1)}), bf16[32,2048,112]{1,2,0:T(8,128)(2,1)}, u32[]{:S(2)}, u32[]{:S(2)}) %all-to-all-start) | async-done | bytes 14680096 | tf_op jit(solution)/shard_map/all_to_all | solution.py:73
  366.1 8.1 %multiply_reduce_fusion = f32[2048]{0:T(1024)S(1)} fusion(bf16[32,2048,112]{1,2,0:T(8,128)(2,1)} %all-to-all-done), kind=kLoop, calls=%fused_computation.3 | loop fusion | flops 22018048 | bytes 14688256 | tf_op jit(solution)/shard_map/reduce_sum | solution.py:50
  374.2 0.0 copy-done
  374.2 0.0 copy-start.1
  374.2 7.0 %fusion.1 = bf16[2048,3584]{0,1:T(8,128)(2,1)S(1)} fusion(f32[3584]{0:T(1024)S(1)} %copy-done, f32[2048]{0:T(1024)S(1)} %add_rsqrt_fusion, bf16[32,2048,112]{1,2,0:T(8,128)(2,1)} %all-to-all-done), kind=kLoop, calls=%fused_computation.2 | loop fusion | flops 29360128 | bytes 29382656 | tf_op jit(solution)/shard_map/convert_element_type | solution.py:51
  381.3 0.0 copy-done.1
  381.3 21.1 %fusion.2 = (f32[2048]{0:T(1024)}, f32[2048]{0:T(1024)S(1)}) fusion(s32[2048]{0:T(1024)S(1)} %copy-done.1, s32[1000]{0:T(1024)S(1)} %iota_add_fusion, bf16[2048,3584]{0,1:T(8,128)(2,1)S(1)} %fusion.1, bf16[1000,3584]{1,0:T(8,128)(2,1)} %param.6), kind=kOutput, calls=%fused_computation.6 | convolution fusion | flops 14692347904 | bytes 21876640 | tf_op jit(solution)/shard_map/vd,td->vt/dot_general | solution.py:57
  402.4 20.4 %all_to_all.35 = f32[8,1,256]{2,1,0:T(1,128)S(1)} all-to-all(f32[8,1,256]{2,1,0:T(1,128)S(1)} %bitcast.19), channel_id=1, replica_groups=mesh['vocab'=32,'seq_0'=4,'seq_1'=2] {'seq_0','seq_1'}, dimensions={0} | all-to-all | bytes 16384 | tf_op jit(solution)/shard_map/all_to_all | solution.py:26
  422.8 3.3 all-to-all-start.1
  426.2 8.8 %all-to-all-done.1 = f32[8,1,256]{2,1,0:T(1,128)S(1)} async-done(((f32[8,1,256]{2,1,0:T(1,128)}), f32[8,1,256]{2,1,0:T(1,128)S(1)}, u32[]{:S(2)}, u32[]{:S(2)}) %all-to-all-start.1) | async-done | bytes 8224 | tf_op jit(solution)/shard_map/all_to_all | solution.py:26
  435.1 14.0 %all_to_all.36 = f32[32,1,512]{2,1,0:T(1,128)S(1)} all-to-all(f32[32,1,512]{2,1,0:T(1,128)S(1)} %broadcast_in_dim.15), channel_id=1, replica_groups=mesh['vocab'=32,'seq_0'=4,'seq_1'=2] {'vocab'}, dimensions={0} | all-to-all | bytes 131072 | tf_op jit(solution)/shard_map/all_to_all | solution.py:32
  449.1 0.1 reduce_sum.77
  449.2 1.2 fusion.4
  450.4 0.6 broadcast_in_dim.16
  451.0 11.3 %all_to_all.37 = f32[8,1,1]{2,1,0:T(1,128)S(1)} all-to-all(f32[8,1,1]{2,1,0:T(1,128)S(1)} %broadcast_in_dim.16), channel_id=1, replica_groups=mesh['vocab'=32,'seq_0'=4,'seq_1'=2] {'seq_0','seq_1'}, dimensions={0} | all-to-all | bytes 64 | tf_op jit(solution)/shard_map/all_to_all | solution.py:32
  462.3 0.6 reduce_sum.79
  (6 shorter events, 0.1 us)
Async XLA Ops:
  28.7 337.4 %all-to-all-start = ((bf16[32,2048,112]{1,2,0:T(8,128)(2,1)}), bf16[32,2048,112]{1,2,0:T(8,128)(2,1)}, u32[]{:S(2)}, u32[]{:S(2)}) async-start(bf16[32,2048,112]{1,2,0:T(8,128)(2,1)} %stack.2), calls=%async_computation | async-start | bytes 29360128 | tf_op jit(solution)/shard_map/all_to_all | solution.py:73
  40.4 333.9 %copy-start = (f32[3584]{0:T(1024)S(1)}, f32[3584]{0:T(1024)}, u32[]{:S(2)}) copy-start(f32[3584]{0:T(1024)} %param.5) | copy-start | bytes 43012
  374.2 7.1 %copy-start.1 = (s32[2048]{0:T(1024)S(1)}, s32[2048]{0:T(1024)}, u32[]{:S(2)}) copy-start(s32[2048]{0:T(1024)} %param.7) | copy-start | bytes 24580
  422.8 12.2 %all-to-all-start.1 = ((f32[8,1,256]{2,1,0:T(1,128)}), f32[8,1,256]{2,1,0:T(1,128)S(1)}, u32[]{:S(2)}, u32[]{:S(2)}) async-start(f32[8,1,256]{2,1,0:T(1,128)} %bitcast.3), calls=%async_computation.1 | async-start | bytes 16384 | tf_op jit(solution)/shard_map/all_to_all | solution.py:26
